TPU v7x, 256 devices: a whole 4x4x8 slice. The times are simulated.
256 devices in a mesh: pts: 32 (over z, y_lo, core), grp: 8 (over y_hi, x).
Axes of the slice: x: 4, y: 4 (y_hi: 2, y_lo: 2; y = y_hi * 2 + y_lo), z: 8, core: 2. Of those that a mesh axis runs over, the one named last changes fastest.
Arguments:
- occ_orbitals: bfloat16 [8192, 1024], P('pts'), may hold values from -0.1875 to 0.1875
- virt_orbitals: bfloat16 [8192, 1024], P('pts'), may hold values from -0.1875 to 0.1875
- columns: bfloat16 [8192, 512], P('pts'), may hold values from -6 to 6
- occ_energies: float32 [1024], replicated, may hold values from -3 to -0.1
- vir_energies: float32 [1024], replicated, may hold values from 0.1 to 3
- tau_index: int32 [8], replicated, may hold values from 0 to 15, as said below
- quad_weights: float32 [8], replicated, may hold values from 0.05 to 0.5
- frequencies: float32 [2], replicated, may hold values from 0.2 to 2
- distance_kept: int32 [32], replicated, may hold values 0 or 1
Outputs:
- response: float32 [2, 512, 8192], P(None, 'grp', 'pts')
Inputs may be any that keep to these rules, and one draw needn't show every extreme that they name: `tau_index`: all entries differ; 0 and 15 are always among them.
All inputs are finite; a program needn't handle non-finite values.
Results may differ from a plain program's by a relative error of at most 0.0026.
Values may be sent and summed in bfloat16 or wider, within the bound.
No kernel may reach another device: no remote copies, remote signals or barrier semaphores. Data moves between devices by JAX's collectives and lax.ppermute only.
A program may use at most 64 MiB of HBM per device.

v0:
```python
import functools
import math

import jax
import jax.numpy as jnp
from jax import lax
from jax.experimental import pallas as pl
from jax.experimental.pallas import tpu as pltpu
from jax.sharding import PartitionSpec as P


AXES = ("pts", "grp")
NZ, NYL, NC, NYH, NX = 8, 2, 2, 2, 4
PLANES = (
    (0, 5, 6, 3, 4, 1, 2, 7),
    (1, 3, 7, 5, 2, 0, 4, 6),
    (2, 6, 4, 1, 7, 3, 5, 0),
    (3, 7, 1, 4, 6, 2, 0, 5),
    (4, 1, 2, 7, 0, 5, 6, 3),
    (5, 0, 3, 6, 1, 4, 7, 2),
    (6, 4, 0, 2, 5, 7, 3, 1),
    (7, 2, 5, 0, 3, 6, 1, 4),
)
TILE = 128
CHUNKS = (64, 64, 64, 64)


def coords(p, g):
    return p // (NYL * NC), p // NC % NYL, p % NC, g // NX, g % NX


def place(z, yl, c, yh, x):
    return (z % NZ * NYL + yl % NYL) * NC + c % NC, yh % NYH * NX + x % NX


def take(array, source):
    found = []
    for p in range(NZ * NYL * NC):
        for g in range(NYH * NX):
            q, h = place(*source(*coords(p, g)))
            found.append((q * NYH * NX + h, p * NYH * NX + g))
    return lax.ppermute(array, AXES, found)


def move_y(z, yl, c, yh, x, by):
    y = (yh * NYL + yl + by) % (NYH * NYL)
    return z, y % NYL, c, y // NYL, x


def from_plane(array):
    return take(array, lambda z, yl, c, yh, x: (PLANES[yh * NX + x][z], yl, c, yh, x))


def from_core(array):
    return take(array, lambda z, yl, c, yh, x: (z, yl, c + 1, yh, x))


def from_y(array, by):
    return take(array, lambda *at: move_y(*at, by))


def scale_kernel(occ_ref, vir_ref, occ_decay_ref, vir_decay_ref, occ_out, vir_out):
    step = 16

    def body(i):
        rows = pl.ds(pl.multiple_of(i * step, step), step)
        for source, decay, out in ((occ_ref, occ_decay_ref, occ_out), (vir_ref, vir_decay_ref, vir_out)):
            values = source[rows, :].astype(jnp.float32)
            for k in range(out.shape[0]):
                out[k, rows, :] = (values * decay[k : k + 1, :]).astype(jnp.bfloat16)

    pl.loop(0, occ_ref.shape[0] // step)(body)


def scaled(occ, vir, occ_decay, vir_decay):
    shape = jax.ShapeDtypeStruct((occ_decay.shape[0], *occ.shape), jnp.bfloat16)
    vmem = pl.BlockSpec(memory_space=pltpu.VMEM)
    return pl.pallas_call(
        scale_kernel,
        out_shape=(shape, shape),
        in_specs=[vmem] * 4,
        out_specs=(vmem, vmem),
        compiler_params=pltpu.CompilerParams(vmem_limit_bytes=16 * 1024 * 1024),
        cost_estimate=pl.CostEstimate(flops=10**8, bytes_accessed=10**7, transcendentals=0),
    )(occ, vir, occ_decay, vir_decay)


def chunk_kernel(segments, n, last, cos_ref, kept_ref, planes_ref, occ_ref, vir_ref, *refs):
    pieces, rest = refs[:n], refs[n:]
    acc_ref = None if len(rest) == 5 else rest[0]
    out_ref, s_occ, s_vir, s_col, parts = rest[-5:]
    taus, points, states = occ_ref.shape
    me = lax.axis_index("pts")
    z, yl, c, yh, x = coords(me, lax.axis_index("grp"))
    at = 0
    for i, first, size, by, other in segments:
        _, s_yl, _, s_yh, _ = move_y(z, yl, c, yh, x, by)
        s_c = 1 - c if other else c
        plane = planes_ref[(s_yh * NX + x) * NZ + z]
        block = (plane * NYL + s_yl) * NC + s_c
        count = kept_ref.shape[0]
        kept = kept_ref[(block - me + count) % count].astype(jnp.float32).astype(jnp.bfloat16)
        here, there = pl.ds(at, size), pl.ds(first, size)
        s_occ[here, :] = pieces[i][there, :states]
        s_vir[here, :] = pieces[i][there, states : 2 * states]
        s_col[here, :] = pieces[i][there, 2 * states :] * kept
        at += size
    contract = (((1,), (1,)), ((), ()))

    def step(i):
        rows = pl.ds(pl.multiple_of(i * TILE, TILE), TILE)
        left = occ_ref[:, rows, :].reshape(taus * TILE, states)
        g_occ = lax.dot_general(left, s_occ[...], contract, preferred_element_type=jnp.float32)
        left = vir_ref[:, rows, :].reshape(taus * TILE, states)
        g_vir = lax.dot_general(left, s_vir[...], contract, preferred_element_type=jnp.float32)
        product = (g_occ * g_vir).reshape(taus, TILE, at)
        for w in range(2):
            chi = cos_ref[w * taus] * product[0]
            for k in range(1, taus):
                chi = chi + cos_ref[w * taus + k] * product[k]
            high = chi.astype(jnp.bfloat16)
            parts[w, 0, rows, :] = high
            parts[w, 1, rows, :] = (chi - high.astype(jnp.float32)).astype(jnp.bfloat16)

    pl.loop(0, points // TILE)(step)
    answers = jnp.dot(parts[...].reshape(4 * points, at), s_col[...], preferred_element_type=jnp.float32)
    answers = answers.reshape(2, 2, points, s_col.shape[1])
    for w in range(2):
        answer = answers[w, 0] + answers[w, 1]
        if acc_ref is not None:
            answer = answer + acc_ref[w]
        if last:
            groups, _, width, _ = out_ref.shape
            out_ref[:, w] = answer.T.astype(jnp.bfloat16).reshape(groups, width, points)
        else:
            out_ref[w] = answer


def chunk_term(cosine, kept, planes, occ_scaled, vir_scaled, pieces, segments, total, last):
    taus, points, states = occ_scaled.shape
    columns = pieces[0].shape[1] - 2 * states
    width = sum(segment[2] for segment in segments)
    if last:
        out = jax.ShapeDtypeStruct((NYH * NX, 2, columns // (NYH * NX), points), jnp.bfloat16)
    else:
        out = jax.ShapeDtypeStruct((2, points, columns), jnp.float32)
    carried = () if total is None else (total,)
    vmem = pl.BlockSpec(memory_space=pltpu.VMEM)
    smem = pl.BlockSpec(memory_space=pltpu.SMEM)
    return pl.pallas_call(
        functools.partial(chunk_kernel, segments, len(pieces), last),
        out_shape=out,
        in_specs=[smem] * 3 + [vmem] * (2 + len(pieces) + len(carried)),
        out_specs=vmem,
        scratch_shapes=[
            pltpu.VMEM((width, states), jnp.bfloat16),
            pltpu.VMEM((width, states), jnp.bfloat16),
            pltpu.VMEM((width, columns), jnp.bfloat16),
            pltpu.VMEM((2, 2, points, width), jnp.bfloat16),
        ],
        compiler_params=pltpu.CompilerParams(vmem_limit_bytes=20 * 1024 * 1024),
        cost_estimate=pl.CostEstimate(
            flops=4 * taus * points * states * width, bytes_accessed=10**7, transcendentals=0
        ),
    )(cosine, kept, planes, occ_scaled, vir_scaled, *pieces, *carried)


def per_device(
    occ_orbitals,
    virt_orbitals,
    columns,
    occ_energies,
    vir_energies,
    tau_index,
    quad_weights,
    frequencies,
    distance_kept,
):
    count = len(CHUNKS)
    arrived, at = [], 0
    for size in CHUNKS:
        part = [a[at : at + size] for a in (occ_orbitals, virt_orbitals, columns)]
        at += size
        arrived.append(from_plane(jnp.concatenate(part, axis=1)))

    times = 0.05 * jnp.exp(tau_index.astype(jnp.float32) * jnp.float32(math.log(1.5)))
    cosine = (-quad_weights[None, :] * jnp.cos(frequencies[:, None] * times[None, :])).reshape(-1)
    occ_decay = jnp.exp(occ_energies[None, :] * times[:, None])
    vir_decay = jnp.exp(-vir_energies[None, :] * times[:, None])
    occ_scaled, vir_scaled = scaled(occ_orbitals, virt_orbitals, occ_decay, vir_decay)
    planes = jnp.array(PLANES, jnp.int32).reshape(-1)

    total = None
    for k, part in enumerate(arrived):
        size = CHUNKS[k]
        last = k == count - 1
        if last:
            half = size // 2
            near = [from_y(part[:half], 1), from_y(part[half:], -1)]
            ways = [(half, 1), (half, -1)]
        else:
            near = [from_y(part, 1 if k % 2 == 0 else -1)]
            ways = [(size, 1 if k % 2 == 0 else -1)]
        beside = from_core(jnp.concatenate([part, *near]))
        pieces = [part, *near, beside]
        segments = [(0, 0, size, 0, False)]
        for i, (rows, by) in enumerate(ways):
            segments.append((1 + i, 0, rows, by, False))
        segments.append((len(pieces) - 1, 0, size, 0, True))
        at = size
        for rows, by in ways:
            segments.append((len(pieces) - 1, at, rows, by, True))
            at += rows
        total = chunk_term(
            cosine, distance_kept, planes, occ_scaled, vir_scaled, pieces, tuple(segments), total, last
        )

    spread = lax.all_to_all(total, "grp", split_axis=0, concat_axis=0, tiled=True)
    return spread.astype(jnp.float32).sum(axis=0)


def solution(mesh):
    placed = (P("pts", None), P("pts", None), P("pts", None), P(), P(), P(), P(), P(), P())
    return jax.shard_map(
        per_device, mesh=mesh, in_specs=placed, out_specs=P(None, "grp", "pts"), check_vma=False
    )
```

profile of v0, /device:TPU:1, one launch (start us, length us, event | category | flops | bytes accessed | tf_op | source)
XLA Modules:
  0.0 96.9 jit_solution(12933425988929200511)
XLA Ops:
  0.0 1.0 fusion.3
  1.0 1.4 %fusion = (bf16[64,1024]{1,0:T(8,128)(2,1)S(1)}, bf16[64,1024]{1,0:T(8,128)(2,1)S(1)}, bf16[64,1024]{1,0:T(8,128)(2,1)S(1)}, bf16[64,1024]{1,0:T(8,128)(2,1)S(1)...) fusion(bf16[256,1024]{1,0:T(8,128)(2,1)} %occ_ref.1, ...), kind=kLoop, calls=%fused_computation.13 | loop fusion | bytes 2097152 | tf_op jit(solution)/shard_map/slice | solution.py:182
  2.3 0.0 copy-start.10
  2.3 0.0 copy-start.8
  2.3 0.0 copy-start.11
  2.4 0.0 copy-start.7
  2.4 0.7 collective-permute-start.10
  3.1 0.7 collective-permute-start.7
  3.8 0.7 collective-permute-start.4
  4.6 0.7 collective-permute-start
  5.3 0.7 multiply_exponential_fusion
  6.0 0.0 collective-permute-done.10.refs_0_
  6.0 20.8 %collective-permute-start.11 = (bf16[64,2560]{1,0:T(8,128)(2,1)S(1)}, bf16[64,2560]{1,0:T(8,128)(2,1)S(1)}, u32[]{:S(2)}, u32[]{:S(2)}) collective-permute-start(bf16[64,2560]{1,0:T(8,128)(2,1)S(1)} %collective-permute-done.10.refs_0_), channel_id=1, source_target_pairs={{16,0},{17,1},{18,2},{19,3},{20,4},{21,5},{22,6},{23,7},{24,8},{25... | collective-permute-start | bytes 983048 | tf_op jit(solution)/shard_map/ppermute | solution.py:42
  26.8 0.0 collective-permute-done.refs_0_
  26.8 16.3 %collective-permute-start.1 = (bf16[32,2560]{1,0:T(8,128)(2,1)S(1)}, bf16[32,2560]{1,0:T(8,128)(2,1)S(1)}, u32[]{:S(2)}, u32[]{:S(2)}) collective-permute-start(bf16[32,2560]{1,0:T(8,128)(2,1)S(1)} %get-tuple-element.18), channel_id=1, source_target_pairs={{16,0},{17,1},{18,2},{19,3},{20,4},{21,5},{22,6},{23,7},{24,8},{25... | collective-permute-start | bytes 491528 | tf_op jit(solution)/shard_map/ppermute | solution.py:42
  43.1 0.0 collective-permute-start.2
  43.1 0.0 collective-permute-done.7.refs_0_
  43.1 0.0 collective-permute-start.8
  43.1 0.0 collective-permute-done.4.refs_0_
  43.1 2.7 %collective-permute-start.5 = (bf16[64,2560]{1,0:T(8,128)(2,1)S(1)}, bf16[64,2560]{1,0:T(8,128)(2,1)S(1)}, u32[]{:S(2)}, u32[]{:S(2)}) collective-permute-start(bf16[64,2560]{1,0:T(8,128)(2,1)S(1)} %collective-permute-done.4.refs_0_), channel_id=1, source_target_pairs={{16,0},{17,1},{18,2},{19,3},{20,4},{21,5},{22,6},{23,7},{24,8},{25... | collective-permute-start | bytes 983048 | tf_op jit(solution)/shard_map/ppermute | solution.py:42
  45.8 0.0 collective-permute-done.11.refs_1_
  45.8 0.9 pad_maximum_fusion.3
  46.7 2.7 %collective-permute-start.12 = (bf16[128,2560]{1,0:T(8,128)(2,1)}, bf16[128,2560]{1,0:T(8,128)(2,1)}, u32[]{:S(2)}, u32[]{:S(2)}) collective-permute-start(bf16[128,2560]{1,0:T(8,128)(2,1)} %pad_maximum_fusion.3), channel_id=1, source_target_pairs={{8,0},{9,1},{10,2},{11,3},{12,4},{13,5},{14,6},{15,7},{0,8},{1,9},... | collective-permute-start | bytes 1966088 | tf_op jit(solution)/shard_map/ppermute | solution.py:42
  49.4 5.6 %collective-permute-done.8.refs_1_ = bf16[64,2560]{1,0:T(8,128)(2,1)S(1)} collective-permute-done((bf16[64,2560]{1,0:T(8,128)(2,1)S(1)}, bf16[64,2560]{1,0:T(8,128)(2,1)S(1)}, u32[]{:S(2)}, u32[]{:S(2)}) %collective-permute-start.8) | collective-permute-done | bytes 327712 | tf_op jit(solution)/shard_map/ppermute | solution.py:42
  55.0 0.9 pad_maximum_fusion.2
  55.9 2.9 %collective-permute-start.9 = (bf16[128,2560]{1,0:T(8,128)(2,1)}, bf16[128,2560]{1,0:T(8,128)(2,1)}, u32[]{:S(2)}, u32[]{:S(2)}) collective-permute-start(bf16[128,2560]{1,0:T(8,128)(2,1)} %pad_maximum_fusion.2), channel_id=1, source_target_pairs={{8,0},{9,1},{10,2},{11,3},{12,4},{13,5},{14,6},{15,7},{0,8},{1,9},... | collective-permute-start | bytes 1966088 | tf_op jit(solution)/shard_map/ppermute | solution.py:42
  58.8 0.0 collective-permute-done.5.refs_1_
  58.8 0.9 pad_maximum_fusion.1
  59.7 0.0 collective-permute-start.6
  59.8 0.0 collective-permute-done.1.refs_1_
  59.8 0.0 collective-permute-done.2.refs_2_
  59.8 0.9 pad_maximum_fusion
  60.7 0.7 copy-done.2
  61.3 0.5 collective-permute-start.3
  61.8 0.1 cosine_multiply_fusion
  61.9 0.1 mul.64.cos_ref
  62.0 0.8 copy-done.4
  62.8 1.3 %shard_map.100 = (bf16[8,256,1024]{2,1,0:T(8,128)(2,1)S(1)}, bf16[8,256,1024]{2,1,0:T(8,128)(2,1)S(1)}) custom-call(bf16[256,1024]{1,0:T(8,128)(2,1)S(1)} %copy-done, bf16[256,1024]{1,0:T(8,128)(2,1)S(1)} %copy-done.1, f32[8,1024]{1,0:T(8,128)S(1)} %copy-done.4, f32[8,1024]{1,0:T(8,128)S(1)} %get-tuple-element.23.vir_decay_ref), custom_call_target="tpu_custom_call" | custom-call | flops 100000000 | bytes 10000000 | tf_op jit(solution)/shard_map/pallas_call | solution.py:78
  64.0 0.0 collective-permute-done.12.refs_2_
  64.1 4.2 %shard_map.101.refs_3_ = f32[2,256,512]{2,1,0:T(8,128)S(1)} custom-call(f32[16]{0:T(128)S(1)} %mul.64.cos_ref, s32[32]{0:T(128)S(1)} %copy-done.5, s32[64]{0:T(128)S(1)} %copy-done.6, bf16[8,256,1024]{2,1,0:T(8,128)(2,1)S(1)} %get-tuple-element.7.occ_ref, bf16[8,256,1024]{2,1,0:T(8,128)(2,1)S(1)} %get-tuple-element.8.vir_ref, ...), custom_call_target="tpu_custom_call" | custom-call | flops 2147483648 | bytes 10000000 | tf_op jit(solution)/shard_map/pallas_call | solution.py:150
  68.3 0.0 collective-permute-done.9.refs_2_
  68.3 4.2 %shard_map.102.refs_3_ = f32[2,256,512]{2,1,0:T(8,128)S(1)} custom-call(f32[16]{0:T(128)S(1)} %mul.64.cos_ref, s32[32]{0:T(128)S(1)} %copy-done.5, s32[64]{0:T(128)S(1)} %copy-done.6, bf16[8,256,1024]{2,1,0:T(8,128)(2,1)S(1)} %get-tuple-element.7.occ_ref, bf16[8,256,1024]{2,1,0:T(8,128)(2,1)S(1)} %get-tuple-element.8.vir_ref, ...), custom_call_target="tpu_custom_call" | custom-call | flops 2147483648 | bytes 10000000 | tf_op jit(solution)/shard_map/pallas_call | solution.py:150
  72.6 0.0 collective-permute-done.6.refs_2_
  72.6 4.3 %shard_map.103.refs_4_ = f32[2,256,512]{2,1,0:T(8,128)S(1)} custom-call(f32[16]{0:T(128)S(1)} %mul.64.cos_ref, s32[32]{0:T(128)S(1)} %copy-done.5, s32[64]{0:T(128)S(1)} %copy-done.6, bf16[8,256,1024]{2,1,0:T(8,128)(2,1)S(1)} %get-tuple-element.7.occ_ref, bf16[8,256,1024]{2,1,0:T(8,128)(2,1)S(1)} %get-tuple-element.8.vir_ref, ...), custom_call_target="tpu_custom_call" | custom-call | flops 2147483648 | bytes 10000000 | tf_op jit(solution)/shard_map/pallas_call | solution.py:150
  76.9 0.0 collective-permute-done.3.refs_3_
  76.9 4.3 %shard_map.104 = bf16[8,2,64,256]{3,2,1,0:T(8,128)(2,1)S(1)} custom-call(f32[16]{0:T(128)S(1)} %mul.64.cos_ref, s32[32]{0:T(128)S(1)} %copy-done.5, s32[64]{0:T(128)S(1)} %copy-done.6, bf16[8,256,1024]{2,1,0:T(8,128)(2,1)S(1)} %get-tuple-element.7.occ_ref, bf16[8,256,1024]{2,1,0:T(8,128)(2,1)S(1)} %get-tuple-element.8.vir_ref, ...), custom_call_target="tpu_custom_call" | custom-call | flops 2147483648 | bytes 10000000 | tf_op jit(solution)/shard_map/pallas_call | solution.py:150
  81.3 14.9 %all_to_all.5 = bf16[8,2,64,256]{3,2,1,0:T(8,128)(2,1)S(1)} all-to-all(bf16[8,2,64,256]{3,2,1,0:T(8,128)(2,1)S(1)} %shard_map.104), channel_id=1, replica_groups=mesh['pts'=32,'grp'=8] {'grp'}, dimensions={0} | all-to-all | bytes 1048576 | tf_op jit(solution)/shard_map/all_to_all | solution.py:218
  96.2 0.7 convert_reduce_fusion
  (26 shorter events, 0.2 us)
Async XLA Ops:
  2.3 2.9 %copy-start.10 = (s32[8]{0:T(128)S(1)}, s32[8]{0:T(128)}, u32[]{:S(2)}) copy-start(s32[8]{0:T(128)} %param.15) | copy-start | bytes 100
  2.3 2.9 %copy-start.8 = (f32[1024]{0:T(1024)S(1)}, f32[1024]{0:T(1024)}, u32[]{:S(2)}) copy-start(f32[1024]{0:T(1024)} %param.14) | copy-start | bytes 12292
  2.3 3.0 %copy-start.11 = (f32[8]{0:T(128)S(1)}, f32[8]{0:T(128)}, u32[]{:S(2)}) copy-start(f32[8]{0:T(128)} %param.16) | copy-start | bytes 100
  2.4 3.0 %copy-start.7 = (f32[1024]{0:T(1024)S(1)}, f32[1024]{0:T(1024)}, u32[]{:S(2)}) copy-start(f32[1024]{0:T(1024)} %param.13) | copy-start | bytes 12292
  2.4 3.6 %collective-permute-start.10 = (bf16[64,2560]{1,0:T(8,128)(2,1)S(1)}, bf16[64,2560]{1,0:T(8,128)(2,1)S(1)}, u32[]{:S(2)}, u32[]{:S(2)}) collective-permute-start(bf16[64,2560]{1,0:T(8,128)(2,1)S(1)} %pad_maximum_fusion.7), channel_id=1, source_target_pairs={{0,0},{33,1},{66,2},{99,3},{132,4},{165,5},{198,6},{231,7},{8,8},{... | collective-permute-start | bytes 983048 | tf_op jit(solution)/shard_map/ppermute | solution.py:42
  3.1 40.0 %collective-permute-start.7 = (bf16[64,2560]{1,0:T(8,128)(2,1)S(1)}, bf16[64,2560]{1,0:T(8,128)(2,1)S(1)}, u32[]{:S(2)}, u32[]{:S(2)}) collective-permute-start(bf16[64,2560]{1,0:T(8,128)(2,1)S(1)} %pad_maximum_fusion.6), channel_id=1, source_target_pairs={{0,0},{33,1},{66,2},{99,3},{132,4},{165,5},{198,6},{231,7},{8,8},{... | collective-permute-start | bytes 983048 | tf_op jit(solution)/shard_map/ppermute | solution.py:42
  3.8 39.2 %collective-permute-start.4 = (bf16[64,2560]{1,0:T(8,128)(2,1)S(1)}, bf16[64,2560]{1,0:T(8,128)(2,1)S(1)}, u32[]{:S(2)}, u32[]{:S(2)}) collective-permute-start(bf16[64,2560]{1,0:T(8,128)(2,1)S(1)} %pad_maximum_fusion.5), channel_id=1, source_target_pairs={{0,0},{33,1},{66,2},{99,3},{132,4},{165,5},{198,6},{231,7},{8,8},{... | collective-permute-start | bytes 983048 | tf_op jit(solution)/shard_map/ppermute | solution.py:42
  4.6 22.2 %collective-permute-start = (bf16[64,2560]{1,0:T(8,128)(2,1)S(1)}, bf16[64,2560]{1,0:T(8,128)(2,1)S(1)}, u32[]{:S(2)}, u32[]{:S(2)}) collective-permute-start(bf16[64,2560]{1,0:T(8,128)(2,1)S(1)} %pad_maximum_fusion.4), channel_id=1, source_target_pairs={{0,0},{33,1},{66,2},{99,3},{132,4},{165,5},{198,6},{231,7},{8,8},{... | collective-permute-start | bytes 983048 | tf_op jit(solution)/shard_map/ppermute | solution.py:42
  6.0 39.8 %collective-permute-start.11 = (bf16[64,2560]{1,0:T(8,128)(2,1)S(1)}, bf16[64,2560]{1,0:T(8,128)(2,1)S(1)}, u32[]{:S(2)}, u32[]{:S(2)}) collective-permute-start(bf16[64,2560]{1,0:T(8,128)(2,1)S(1)} %collective-permute-done.10.refs_0_), channel_id=1, source_target_pairs={{16,0},{17,1},{18,2},{19,3},{20,4},{21,5},{22,6},{23,7},{24,8},{25... | collective-permute-start | bytes 983048 | tf_op jit(solution)/shard_map/ppermute | solution.py:42
  26.8 32.9 %collective-permute-start.1 = (bf16[32,2560]{1,0:T(8,128)(2,1)S(1)}, bf16[32,2560]{1,0:T(8,128)(2,1)S(1)}, u32[]{:S(2)}, u32[]{:S(2)}) collective-permute-start(bf16[32,2560]{1,0:T(8,128)(2,1)S(1)} %get-tuple-element.18), channel_id=1, source_target_pairs={{16,0},{17,1},{18,2},{19,3},{20,4},{21,5},{22,6},{23,7},{24,8},{25... | collective-permute-start | bytes 491528 | tf_op jit(solution)/shard_map/ppermute | solution.py:42
  43.1 16.7 %collective-permute-start.2 = (bf16[32,2560]{1,0:T(8,128)(2,1)S(1)}, bf16[32,2560]{1,0:T(8,128)(2,1)S(1)}, u32[]{:S(2)}, u32[]{:S(2)}) collective-permute-start(bf16[32,2560]{1,0:T(8,128)(2,1)S(1)} %get-tuple-element.17), channel_id=1, source_target_pairs={{20,0},{21,1},{22,2},{23,3},{16,4},{17,5},{18,6},{19,7},{28,8},{29... | collective-permute-start | bytes 491528 | tf_op jit(solution)/shard_map/ppermute | solution.py:42
  43.1 11.9 %collective-permute-start.8 = (bf16[64,2560]{1,0:T(8,128)(2,1)S(1)}, bf16[64,2560]{1,0:T(8,128)(2,1)S(1)}, u32[]{:S(2)}, u32[]{:S(2)}) collective-permute-start(bf16[64,2560]{1,0:T(8,128)(2,1)S(1)} %collective-permute-done.7.refs_0_), channel_id=1, source_target_pairs={{20,0},{21,1},{22,2},{23,3},{16,4},{17,5},{18,6},{19,7},{28,8},{29... | collective-permute-start | bytes 983048 | tf_op jit(solution)/shard_map/ppermute | solution.py:42
  43.1 15.7 %collective-permute-start.5 = (bf16[64,2560]{1,0:T(8,128)(2,1)S(1)}, bf16[64,2560]{1,0:T(8,128)(2,1)S(1)}, u32[]{:S(2)}, u32[]{:S(2)}) collective-permute-start(bf16[64,2560]{1,0:T(8,128)(2,1)S(1)} %collective-permute-done.4.refs_0_), channel_id=1, source_target_pairs={{16,0},{17,1},{18,2},{19,3},{20,4},{21,5},{22,6},{23,7},{24,8},{25... | collective-permute-start | bytes 983048 | tf_op jit(solution)/shard_map/ppermute | solution.py:42
  46.7 17.3 %collective-permute-start.12 = (bf16[128,2560]{1,0:T(8,128)(2,1)}, bf16[128,2560]{1,0:T(8,128)(2,1)}, u32[]{:S(2)}, u32[]{:S(2)}) collective-permute-start(bf16[128,2560]{1,0:T(8,128)(2,1)} %pad_maximum_fusion.3), channel_id=1, source_target_pairs={{8,0},{9,1},{10,2},{11,3},{12,4},{13,5},{14,6},{15,7},{0,8},{1,9},... | collective-permute-start | bytes 1966088 | tf_op jit(solution)/shard_map/ppermute | solution.py:42
  55.9 5.9 %copy-start.9 = (f32[2]{0:T(128)S(1)}, f32[2]{0:T(128)}, u32[]{:S(2)}) copy-start(f32[2]{0:T(128)} %param.17) | copy-start | bytes 28
  55.9 6.1 %copy-start = (bf16[256,1024]{1,0:T(8,128)(2,1)S(1)}, bf16[256,1024]{1,0:T(8,128)(2,1)}, u32[]{:S(2)}) copy-start(bf16[256,1024]{1,0:T(8,128)(2,1)} %occ_ref.1) | copy-start | bytes 1572868
  55.9 6.1 %copy-start.1 = (bf16[256,1024]{1,0:T(8,128)(2,1)S(1)}, bf16[256,1024]{1,0:T(8,128)(2,1)}, u32[]{:S(2)}) copy-start(bf16[256,1024]{1,0:T(8,128)(2,1)} %vir_ref.1) | copy-start | bytes 1572868
  55.9 12.5 %collective-permute-start.9 = (bf16[128,2560]{1,0:T(8,128)(2,1)}, bf16[128,2560]{1,0:T(8,128)(2,1)}, u32[]{:S(2)}, u32[]{:S(2)}) collective-permute-start(bf16[128,2560]{1,0:T(8,128)(2,1)} %pad_maximum_fusion.2), channel_id=1, source_target_pairs={{8,0},{9,1},{10,2},{11,3},{12,4},{13,5},{14,6},{15,7},{0,8},{1,9},... | collective-permute-start | bytes 1966088 | tf_op jit(solution)/shard_map/ppermute | solution.py:42
  59.7 4.3 %copy-start.5 = (s32[32]{0:T(128)S(1)}, s32[32]{0:T(128)}, u32[]{:S(2)}) copy-start(s32[32]{0:T(128)} %kept_ref.7) | copy-start | bytes 388
  59.7 4.3 %copy-start.6 = (s32[64]{0:T(128)S(1)}, s32[64]{0:T(128)}, u32[]{:S(2)}) copy-start(s32[64]{0:T(128)} %constant.9.planes_ref) | copy-start | bytes 772
  59.7 12.9 %collective-permute-start.6 = (bf16[128,2560]{1,0:T(8,128)(2,1)}, bf16[128,2560]{1,0:T(8,128)(2,1)}, u32[]{:S(2)}, u32[]{:S(2)}) collective-permute-start(bf16[128,2560]{1,0:T(8,128)(2,1)} %pad_maximum_fusion.1), channel_id=1, source_target_pairs={{8,0},{9,1},{10,2},{11,3},{12,4},{13,5},{14,6},{15,7},{0,8},{1,9},... | collective-permute-start | bytes 1966088 | tf_op jit(solution)/shard_map/ppermute | solution.py:42
  60.6 0.7 copy-start.2
  61.3 15.6 %collective-permute-start.3 = (bf16[128,2560]{1,0:T(8,128)(2,1)}, bf16[128,2560]{1,0:T(8,128)(2,1)}, u32[]{:S(2)}, u32[]{:S(2)}) collective-permute-start(bf16[128,2560]{1,0:T(8,128)(2,1)} %pad_maximum_fusion), channel_id=1, source_target_pairs={{8,0},{9,1},{10,2},{11,3},{12,4},{13,5},{14,6},{15,7},{0,8},{1,9},... | collective-permute-start | bytes 1966088 | tf_op jit(solution)/shard_map/ppermute | solution.py:42
  62.0 0.8 copy-start.4
  72.6 4.3 %copy-start.3 = (bf16[32,2560]{1,0:T(8,128)(2,1)S(1)}, bf16[32,2560]{1,0:T(8,128)(2,1)}, u32[]{:S(2)}) copy-start(bf16[32,2560]{1,0:T(8,128)(2,1)} %copy-done.2) | copy-start | bytes 491524
where the time goes:
time: 97.5 us; the launch traced here: 96.9 us
  starting transfers between devices  48.6 us (50%)
  Pallas kernels  18.4 us (19%)
  blocking collectives  14.9 us (15%)
  waiting for transfers between devices  5.63 us (6%)
  other arithmetic  5.22 us (5%)
  local copies, waits for them, and re-layouts  3.89 us (4%)
    ppermute x13, starting transfers between devices, take(): return lax.ppermute(array, AXES, found)  48.6 us
    pallas_call x4, Pallas kernels, chunk_term(): pl.pallas_call(functools.partial(chunk_kernel, segments, len(pieces), las...  17.1 us
    all_to_all x1, blocking collectives, per_device(): lax.all_to_all(total, 'grp', split_axis=0, concat_axis=0, tiled=True)  14.9 us
    ppermute x13, waiting for transfers between devices, take(): return lax.ppermute(array, AXES, found)  5.63 us
    concatenate x4, other arithmetic, per_device(): beside = from_core(jnp.concatenate([part, *near]))  3.57 us
    slice x2, local copies, waits for them, and re-layouts, per_device(): part = [a[at:at + size] for a in (occ_orbitals, virt_orbitals, columns)]  2.31 us
  transfers between devices with their start and end apart: 13, of which 1 were waited for; matrix products, arithmetic and copies ran while one was open for 5% of the time, Pallas kernels for 15%

commit v1 on v0

v1 whole, which is shorter than its diff:
```python
import functools
import math

import jax
import jax.numpy as jnp
from jax import lax
from jax.experimental import pallas as pl
from jax.experimental.pallas import tpu as pltpu
from jax.sharding import PartitionSpec as P


AXES = ("pts", "grp")
NZ, NYL, NC, NYH, NX = 8, 2, 2, 2, 4
PLANES = (
    (0, 5, 6, 3, 4, 1, 2, 7),
    (1, 3, 7, 5, 2, 0, 4, 6),
    (2, 6, 4, 1, 7, 3, 5, 0),
    (3, 7, 1, 4, 6, 2, 0, 5),
    (4, 1, 2, 7, 0, 5, 6, 3),
    (5, 0, 3, 6, 1, 4, 7, 2),
    (6, 4, 0, 2, 5, 7, 3, 1),
    (7, 2, 5, 0, 3, 6, 1, 4),
)
TILE = 128
CHUNKS = (128, 64, 64)


def coords(p, g):
    return p // (NYL * NC), p // NC % NYL, p % NC, g // NX, g % NX


def place(z, yl, c, yh, x):
    return (z % NZ * NYL + yl % NYL) * NC + c % NC, yh % NYH * NX + x % NX


def take(array, source):
    found = []
    for p in range(NZ * NYL * NC):
        for g in range(NYH * NX):
            q, h = place(*source(*coords(p, g)))
            found.append((q * NYH * NX + h, p * NYH * NX + g))
    return lax.ppermute(array, AXES, found)


def move_y(z, yl, c, yh, x, by):
    y = (yh * NYL + yl + by) % (NYH * NYL)
    return z, y % NYL, c, y // NYL, x


def from_plane(array):
    return take(array, lambda z, yl, c, yh, x: (PLANES[yh * NX + x][z], yl, c, yh, x))


def from_core(array):
    return take(array, lambda z, yl, c, yh, x: (z, yl, c + 1, yh, x))


def from_y(array, by):
    return take(array, lambda *at: move_y(*at, by))


def pack_kernel(occ_ref, vir_ref, col_ref, *refs):
    outs, sems = refs[:-1], refs[-1]
    copies, at = [], 0
    for out in outs:
        size, left = out.shape[0], 0
        for source in (occ_ref, vir_ref, col_ref):
            width = source.shape[1]
            copies.append(
                pltpu.make_async_copy(
                    source.at[pl.ds(at, size), :], out.at[:, pl.ds(left, width)], sems.at[len(copies)]
                )
            )
            left += width
        at += size
    for copy in copies:
        copy.start()
    for copy in copies:
        copy.wait()


def packed(occ, vir, col):
    width = occ.shape[1] + vir.shape[1] + col.shape[1]
    vmem = pl.BlockSpec(memory_space=pltpu.VMEM)
    return pl.pallas_call(
        pack_kernel,
        out_shape=[jax.ShapeDtypeStruct((size, width), jnp.bfloat16) for size in CHUNKS],
        in_specs=[pl.BlockSpec(memory_space=pltpu.HBM)] * 3,
        out_specs=[vmem] * len(CHUNKS),
        scratch_shapes=[pltpu.SemaphoreType.DMA((3 * len(CHUNKS),))],
        compiler_params=pltpu.CompilerParams(vmem_limit_bytes=65000000),
        cost_estimate=pl.CostEstimate(flops=10**6, bytes_accessed=3 * 10**6, transcendentals=0),
    )(occ, vir, col)


def join_kernel(*refs):
    *pieces, out = refs
    at = 0
    for piece in pieces:
        out[pl.ds(at, piece.shape[0]), :] = piece[...]
        at += piece.shape[0]


def split_kernel(piece, *outs):
    at = 0
    for out in outs:
        out[...] = piece[pl.ds(at, out.shape[0]), :]
        at += out.shape[0]


def moved(kernel, pieces, sizes):
    vmem = pl.BlockSpec(memory_space=pltpu.VMEM)
    return pl.pallas_call(
        kernel,
        out_shape=[jax.ShapeDtypeStruct((size, pieces[0].shape[1]), pieces[0].dtype) for size in sizes],
        in_specs=[vmem] * len(pieces),
        out_specs=[vmem] * len(sizes),
        compiler_params=pltpu.CompilerParams(vmem_limit_bytes=8 * 1024 * 1024),
        cost_estimate=pl.CostEstimate(flops=10**6, bytes_accessed=10**6, transcendentals=0),
    )(*pieces)


def scale_kernel(
    sources, cos_ref, kept_ref, planes_ref, occ_ref, vir_ref, occ_decay_ref, vir_decay_ref,
    occ_out, vir_out, cos_out, kept_out,
):
    me = lax.axis_index("pts")
    z, yl, c, yh, x = coords(me, lax.axis_index("grp"))
    count = kept_ref.shape[0]
    for i, (by, other) in enumerate(sources):
        _, s_yl, _, s_yh, _ = move_y(z, yl, c, yh, x, by)
        s_c = 1 - c if other else c
        plane = planes_ref[(s_yh * NX + x) * NZ + z]
        block = (plane * NYL + s_yl) * NC + s_c
        kept = kept_ref[(block - me + count) % count].astype(jnp.float32)
        kept_out[i : i + 1, :] = jnp.full((1, kept_out.shape[1]), kept, jnp.float32)
    for i in range(cos_out.shape[0]):
        cos_out[i : i + 1, :] = jnp.full((1, cos_out.shape[1]), cos_ref[i], jnp.float32)
    step = 16

    def body(i):
        rows = pl.ds(pl.multiple_of(i * step, step), step)
        for source, decay, out in ((occ_ref, occ_decay_ref, occ_out), (vir_ref, vir_decay_ref, vir_out)):
            values = source[rows, :].astype(jnp.float32)
            for k in range(out.shape[0]):
                out[k, rows, :] = (values * decay[k : k + 1, :]).astype(jnp.bfloat16)

    pl.loop(0, occ_ref.shape[0] // step)(body)


SOURCES = ((0, False), (0, True), (1, False), (1, True), (-1, False), (-1, True))


def scaled(cosine, kept, planes, occ, vir, occ_decay, vir_decay, columns):
    shape = jax.ShapeDtypeStruct((occ_decay.shape[0], *occ.shape), jnp.bfloat16)
    rows = jax.ShapeDtypeStruct((cosine.shape[0], 256), jnp.float32)
    marks = jax.ShapeDtypeStruct((8, columns), jnp.float32)
    vmem = pl.BlockSpec(memory_space=pltpu.VMEM)
    smem = pl.BlockSpec(memory_space=pltpu.SMEM)
    return pl.pallas_call(
        functools.partial(scale_kernel, SOURCES),
        out_shape=(shape, shape, rows, marks),
        in_specs=[smem] * 3 + [vmem] * 4,
        out_specs=(vmem,) * 4,
        compiler_params=pltpu.CompilerParams(vmem_limit_bytes=16 * 1024 * 1024),
        cost_estimate=pl.CostEstimate(flops=10**8, bytes_accessed=10**7, transcendentals=0),
    )(cosine, kept, planes, occ, vir, occ_decay, vir_decay)


def chunk_kernel(segments, n, last, cos_ref, kept_ref, occ_ref, vir_ref, *refs):
    pieces, rest = refs[:n], refs[n:]
    acc_ref = None if len(rest) == 5 else rest[0]
    out_ref, s_occ, s_vir, s_col, parts = rest[-5:]
    taus, points, states = occ_ref.shape
    at = 0
    for i, first, size, kind in segments:
        here, there = pl.ds(at, size), pl.ds(first, size)
        s_occ[here, :] = pieces[i][there, :states]
        s_vir[here, :] = pieces[i][there, states : 2 * states]
        s_col[here, :] = pieces[i][there, 2 * states :] * kept_ref[kind : kind + 1, :].astype(jnp.bfloat16)
        at += size
    contract = (((1,), (1,)), ((), ()))

    def step(i):
        rows = pl.ds(pl.multiple_of(i * TILE, TILE), TILE)
        left = occ_ref[:, rows, :].reshape(taus * TILE, states)
        g_occ = lax.dot_general(left, s_occ[...], contract, preferred_element_type=jnp.float32)
        left = vir_ref[:, rows, :].reshape(taus * TILE, states)
        g_vir = lax.dot_general(left, s_vir[...], contract, preferred_element_type=jnp.float32)
        product = (g_occ * g_vir).reshape(taus, TILE, at)
        for w in range(2):
            chi = cos_ref[w * taus : w * taus + 1, :] * product[0]
            for k in range(1, taus):
                chi = chi + cos_ref[w * taus + k : w * taus + k + 1, :] * product[k]
            high = chi.astype(jnp.bfloat16)
            parts[w, 0, rows, :] = high
            parts[w, 1, rows, :] = (chi - high.astype(jnp.float32)).astype(jnp.bfloat16)

    pl.loop(0, points // TILE)(step)
    answers = jnp.dot(parts[...].reshape(4 * points, at), s_col[...], preferred_element_type=jnp.float32)
    answers = answers.reshape(2, 2, points, s_col.shape[1])
    for w in range(2):
        answer = answers[w, 0] + answers[w, 1]
        if acc_ref is not None:
            answer = answer + acc_ref[w]
        if last:
            groups, _, width, _ = out_ref.shape
            out_ref[:, w] = answer.T.astype(jnp.bfloat16).reshape(groups, width, points)
        else:
            out_ref[w] = answer


def chunk_term(cosine, kept, occ_scaled, vir_scaled, pieces, segments, total, last):
    taus, points, states = occ_scaled.shape
    columns = pieces[0].shape[1] - 2 * states
    width = sum(segment[2] for segment in segments)
    if last:
        out = jax.ShapeDtypeStruct((NYH * NX, 2, columns // (NYH * NX), points), jnp.bfloat16)
    else:
        out = jax.ShapeDtypeStruct((2, points, columns), jnp.float32)
    carried = () if total is None else (total,)
    vmem = pl.BlockSpec(memory_space=pltpu.VMEM)
    return pl.pallas_call(
        functools.partial(chunk_kernel, segments, len(pieces), last),
        out_shape=out,
        in_specs=[vmem] * (4 + len(pieces) + len(carried)),
        out_specs=vmem,
        scratch_shapes=[
            pltpu.VMEM((width, states), jnp.bfloat16),
            pltpu.VMEM((width, states), jnp.bfloat16),
            pltpu.VMEM((width, columns), jnp.bfloat16),
            pltpu.VMEM((2, 2, points, width), jnp.bfloat16),
        ],
        compiler_params=pltpu.CompilerParams(vmem_limit_bytes=20 * 1024 * 1024),
        cost_estimate=pl.CostEstimate(
            flops=4 * taus * points * states * width, bytes_accessed=10**7, transcendentals=0
        ),
    )(cosine, kept, occ_scaled, vir_scaled, *pieces, *carried)


def per_device(
    occ_orbitals,
    virt_orbitals,
    columns,
    occ_energies,
    vir_energies,
    tau_index,
    quad_weights,
    frequencies,
    distance_kept,
):
    parts = packed(occ_orbitals, virt_orbitals, columns)
    arrived = []
    for part in parts:
        arrived.append(from_plane(part))

    times = 0.05 * jnp.exp(tau_index.astype(jnp.float32) * jnp.float32(math.log(1.5)))
    cosine = (-quad_weights[None, :] * jnp.cos(frequencies[:, None] * times[None, :])).reshape(-1)
    occ_decay = jnp.exp(occ_energies[None, :] * times[:, None])
    vir_decay = jnp.exp(-vir_energies[None, :] * times[:, None])
    planes = jnp.array(PLANES, jnp.int32).reshape(-1)
    occ_scaled, vir_scaled, cos_rows, marks = scaled(
        cosine, distance_kept, planes, occ_orbitals, virt_orbitals, occ_decay, vir_decay, columns.shape[1]
    )

    def exchanged(k, sizes, steps):
        part = arrived[k]
        halves = moved(split_kernel, [part], sizes) if len(sizes) > 1 else [part]
        near = [from_y(half, by) for half, by in zip(halves, steps)]
        (joined,) = moved(join_kernel, [part, *near], [part.shape[0] + sum(sizes)])
        beside = from_core(joined)
        return [part, *near, beside]

    a = exchanged(0, (64, 64), (1, -1))
    b = exchanged(1, (64,), (1,))
    c = exchanged(2, (32, 32), (1, -1))
    work = (
        ((a[0], a[1], a[3]), ((0, 0, 64, 0), (1, 0, 64, 2), (2, 0, 64, 1), (2, 128, 64, 3))),
        ((a[0], a[2], a[3]), ((0, 64, 64, 0), (1, 0, 64, 4), (2, 64, 64, 1), (2, 192, 64, 5))),
        ((b[0], b[1], b[2]), ((0, 0, 64, 0), (1, 0, 64, 2), (2, 0, 64, 1), (2, 64, 64, 3))),
        (
            (c[0], c[1], c[2], c[3]),
            ((0, 0, 64, 0), (1, 0, 32, 2), (2, 0, 32, 4), (3, 0, 64, 1), (3, 64, 32, 3), (3, 96, 32, 5)),
        ),
    )
    total = None
    for k, (pieces, segments) in enumerate(work):
        total = chunk_term(
            cos_rows, marks, occ_scaled, vir_scaled, pieces, segments, total, k == len(work) - 1
        )

    spread = lax.all_to_all(total, "grp", split_axis=0, concat_axis=0, tiled=True)
    return spread.astype(jnp.float32).sum(axis=0)


def solution(mesh):
    placed = (P("pts", None), P("pts", None), P("pts", None), P(), P(), P(), P(), P(), P())
    return jax.shard_map(per_device, mesh=mesh, in_specs=placed, out_specs=P(None, "grp", "pts"), check_vma=False)
```

time: 97.5 us -> 108 us (1.11)
  starting transfers between devices: 48.6 us -> 57.7 us
  Pallas kernels: 18.4 us -> 22.4 us
  other arithmetic: 5.22 us -> 1.54 us
  waiting for transfers between devices: 5.63 us -> 9.04 us
  local copies, waits for them, and re-layouts: 3.89 us -> 2.55 us
    ppermute x13 -> x11, starting transfers between devices: 48.6 us -> 57.7 us  [take(): return lax.ppermute(array, AXES, found)]
    pallas_call x1 -> x7, Pallas kernels: 1.27 us -> 7.55 us  [the longest x5 3.17 us: moved(): pl.pallas_call(kernel, out_shape=[jax.ShapeDtypeStruct((size, pieces[0].s...]
    concatenate x8 -> x0, other arithmetic: 3.67 us -> none  [the longest x4 3.57 us: per_device(): beside = from_core(jnp.concatenate([part, *near]))]
    ppermute x13 -> x11, waiting for transfers between devices: 5.63 us -> 9.04 us  [take(): return lax.ppermute(array, AXES, found)]
    slice x3 -> x0, local copies, waits for them, and re-layouts: 2.33 us -> none  [the longest x2 2.31 us: per_device(): part = [a[at:at + size] for a in (occ_orbitals, virt_orbitals, columns)]]
    pallas_call x4, Pallas kernels: 17.1 us -> 14.8 us  [chunk_term(): pl.pallas_call(functools.partial(chunk_kernel, segments, len(pieces), las...]
    unnamed x24 -> x40, local copies, waits for them, and re-layouts: 1.47 us -> 2.46 us
  transfers between devices with their start and end apart: 13 -> 11, of which waited for: 1 -> 2; matrix products, arithmetic and copies ran while one was open for 5% -> 1% of each run, Pallas kernels for 15% -> 13%
where the time goes in v1:
time: 108 us; the launch traced here: 107 us
  starting transfers between devices  57.7 us (53%)
  Pallas kernels  22.4 us (21%)
  blocking collectives  14 us (13%)
  waiting for transfers between devices  9.04 us (8%)
  local copies, waits for them, and re-layouts  2.55 us (2%)
  other arithmetic  1.54 us (1%)
    ppermute x11, starting transfers between devices, take(): return lax.ppermute(array, AXES, found)  57.7 us
    pallas_call x4, Pallas kernels, chunk_term(): pl.pallas_call(functools.partial(chunk_kernel, segments, len(pieces), las...  14.8 us
    all_to_all x1, blocking collectives, per_device(): lax.all_to_all(total, 'grp', split_axis=0, concat_axis=0, tiled=True)  14 us
    ppermute x11, waiting for transfers between devices, take(): return lax.ppermute(array, AXES, found)  9.04 us
    pallas_call x5, Pallas kernels, moved(): pl.pallas_call(kernel, out_shape=[jax.ShapeDtypeStruct((size, pieces[0].s...  3.17 us
    unnamed x40, local copies, waits for them, and re-layouts  2.46 us
    pallas_call x1, Pallas kernels, packed(): pl.pallas_call(pack_kernel, out_shape=[jax.ShapeDtypeStruct((size, width)...  2.46 us
  transfers between devices with their start and end apart: 11, of which 2 were waited for; matrix products, arithmetic and copies ran while one was open for 1% of the time, Pallas kernels for 13%

profile of v1, /device:TPU:1, one launch (start us, length us, event | category | flops | bytes accessed | tf_op | source)
XLA Modules:
  0.0 107.4 jit_solution(13548606851232543656)
XLA Ops:
  0.0 0.0 copy-start.16
  0.0 0.0 copy-start.18
  0.1 2.5 %shard_map.101 = (bf16[128,2560]{1,0:T(8,128)(2,1)}, bf16[64,2560]{1,0:T(8,128)(2,1)}, bf16[64,2560]{1,0:T(8,128)(2,1)}) custom-call(bf16[256,1024]{1,0:T(8,128)(2,1)} %occ_ref.3, bf16[256,1024]{1,0:T(8,128)(2,1)} %vir_ref.3, bf16[256,512]{1,0:T(8,128)(2,1)} %col_ref.1), custom_call_target="tpu_custom_call" | custom-call | flops 1000000 | bytes 3000000 | tf_op jit(solution)/shard_map/pallas_call | solution.py:85
  2.5 0.0 copy-start.17
  2.5 1.7 %collective-permute-start.7 = (bf16[128,2560]{1,0:T(8,128)(2,1)}, bf16[128,2560]{1,0:T(8,128)(2,1)S(1)}, u32[]{:S(2)}, u32[]{:S(2)}) collective-permute-start(bf16[128,2560]{1,0:T(8,128)(2,1)} %get-tuple-element.24), channel_id=1, source_target_pairs={{0,0},{33,1},{66,2},{99,3},{132,4},{165,5},{198,6},{231,7},{8,8},{... | collective-permute-start | bytes 1966088 | tf_op jit(solution)/shard_map/ppermute | solution.py:42
  4.3 0.0 collective-permute-done.7.piece.refs_0_
  4.3 2.2 %collective-permute-start.8 = (bf16[64,2560]{1,0:T(8,128)(2,1)S(1)}, bf16[64,2560]{1,0:T(8,128)(2,1)S(1)}, u32[]{:S(2)}, u32[]{:S(2)}) collective-permute-start(bf16[64,2560]{1,0:T(8,128)(2,1)S(1)} %get-tuple-element.25), channel_id=1, source_target_pairs={{20,0},{21,1},{22,2},{23,3},{16,4},{17,5},{18,6},{19,7},{28,8},{29... | collective-permute-start | bytes 983048 | tf_op jit(solution)/shard_map/ppermute | solution.py:42
  6.5 23.2 %collective-permute-start.9 = (bf16[64,2560]{1,0:T(8,128)(2,1)S(1)}, bf16[64,2560]{1,0:T(8,128)(2,1)S(1)}, u32[]{:S(2)}, u32[]{:S(2)}) collective-permute-start(bf16[64,2560]{1,0:T(8,128)(2,1)S(1)} %get-tuple-element.26), channel_id=1, source_target_pairs={{16,0},{17,1},{18,2},{19,3},{20,4},{21,5},{22,6},{23,7},{24,8},{25... | collective-permute-start | bytes 983048 | tf_op jit(solution)/shard_map/ppermute | solution.py:42
  29.8 6.7 %collective-permute-done.8.refs_2_.refs_1_ = bf16[64,2560]{1,0:T(8,128)(2,1)S(1)} collective-permute-done((bf16[64,2560]{1,0:T(8,128)(2,1)S(1)}, bf16[64,2560]{1,0:T(8,128)(2,1)S(1)}, u32[]{:S(2)}, u32[]{:S(2)}) %collective-permute-start.8) | collective-permute-done | bytes 327712 | tf_op jit(solution)/shard_map/ppermute | solution.py:42
  36.5 0.0 collective-permute-done.9.refs_1_
  36.5 1.3 %shard_map.106 = bf16[256,2560]{1,0:T(8,128)(2,1)} custom-call(bf16[128,2560]{1,0:T(8,128)(2,1)S(1)} %collective-permute-done.7.piece.refs_0_, bf16[64,2560]{1,0:T(8,128)(2,1)S(1)} %collective-permute-done.9.refs_1_, bf16[64,2560]{1,0:T(8,128)(2,1)S(1)} %collective-permute-done.8.refs_2_.refs_1_), custom_call_target="tpu_custom_call" | custom-call | flops 1000000 | bytes 1000000 | tf_op jit(solution)/shard_map/pallas_call | solution.py:113
  37.8 1.8 %collective-permute-start.10 = (bf16[256,2560]{1,0:T(8,128)(2,1)}, bf16[256,2560]{1,0:T(8,128)(2,1)S(1)}, u32[]{:S(2)}, u32[]{:S(2)}) collective-permute-start(bf16[256,2560]{1,0:T(8,128)(2,1)} %shard_map.106), channel_id=1, source_target_pairs={{8,0},{9,1},{10,2},{11,3},{12,4},{13,5},{14,6},{15,7},{0,8},{1,9},... | collective-permute-start | bytes 3932168 | tf_op jit(solution)/shard_map/ppermute | solution.py:42
  39.6 1.6 %collective-permute-start.4 = (bf16[64,2560]{1,0:T(8,128)(2,1)}, bf16[64,2560]{1,0:T(8,128)(2,1)S(1)}, u32[]{:S(2)}, u32[]{:S(2)}) collective-permute-start(bf16[64,2560]{1,0:T(8,128)(2,1)} %get-tuple-element.23), channel_id=1, source_target_pairs={{0,0},{33,1},{66,2},{99,3},{132,4},{165,5},{198,6},{231,7},{8,8},{... | collective-permute-start | bytes 983048 | tf_op jit(solution)/shard_map/ppermute | solution.py:42
  41.2 0.0 copy-done.4
  41.2 1.6 %collective-permute-start = (bf16[64,2560]{1,0:T(8,128)(2,1)}, bf16[64,2560]{1,0:T(8,128)(2,1)S(1)}, u32[]{:S(2)}, u32[]{:S(2)}) collective-permute-start(bf16[64,2560]{1,0:T(8,128)(2,1)} %get-tuple-element.20), channel_id=1, source_target_pairs={{0,0},{33,1},{66,2},{99,3},{132,4},{165,5},{198,6},{231,7},{8,8},{... | collective-permute-start | bytes 983048 | tf_op jit(solution)/shard_map/ppermute | solution.py:42
  42.9 0.0 collective-permute-done.4.refs_0_
  42.9 14.7 %collective-permute-start.5 = (bf16[64,2560]{1,0:T(8,128)(2,1)S(1)}, bf16[64,2560]{1,0:T(8,128)(2,1)S(1)}, u32[]{:S(2)}, u32[]{:S(2)}) collective-permute-start(bf16[64,2560]{1,0:T(8,128)(2,1)S(1)} %collective-permute-done.4.refs_0_), channel_id=1, source_target_pairs={{16,0},{17,1},{18,2},{19,3},{20,4},{21,5},{22,6},{23,7},{24,8},{25... | collective-permute-start | bytes 983048 | tf_op jit(solution)/shard_map/ppermute | solution.py:42
  57.5 0.0 copy-done.18
  57.6 0.0 collective-permute-done.piece.refs_0_
  57.6 6.8 %collective-permute-start.1 = (bf16[32,2560]{1,0:T(8,128)(2,1)S(1)}, bf16[32,2560]{1,0:T(8,128)(2,1)S(1)}, u32[]{:S(2)}, u32[]{:S(2)}) collective-permute-start(bf16[32,2560]{1,0:T(8,128)(2,1)S(1)} %get-tuple-element.21), channel_id=1, source_target_pairs={{16,0},{17,1},{18,2},{19,3},{20,4},{21,5},{22,6},{23,7},{24,8},{25... | collective-permute-start | bytes 491528 | tf_op jit(solution)/shard_map/ppermute | solution.py:42
  64.4 0.0 collective-permute-start.2
  64.4 0.0 collective-permute-done.5.refs_1_
  64.4 1.0 shard_map.104
  65.4 1.4 %collective-permute-start.6 = (bf16[128,2560]{1,0:T(8,128)(2,1)}, bf16[128,2560]{1,0:T(8,128)(2,1)}, u32[]{:S(2)}, u32[]{:S(2)}) collective-permute-start(bf16[128,2560]{1,0:T(8,128)(2,1)} %shard_map.104), channel_id=1, source_target_pairs={{8,0},{9,1},{10,2},{11,3},{12,4},{13,5},{14,6},{15,7},{0,8},{1,9},... | collective-permute-start | bytes 1966088 | tf_op jit(solution)/shard_map/ppermute | solution.py:42
  66.8 0.7 multiply_exponential_fusion
  67.5 0.0 collective-permute-done.1.refs_1_
  67.5 2.3 %collective-permute-done.2.refs_2_ = bf16[32,2560]{1,0:T(8,128)(2,1)S(1)} collective-permute-done((bf16[32,2560]{1,0:T(8,128)(2,1)S(1)}, bf16[32,2560]{1,0:T(8,128)(2,1)S(1)}, u32[]{:S(2)}, u32[]{:S(2)}) %collective-permute-start.2) | collective-permute-done | bytes 163872 | tf_op jit(solution)/shard_map/ppermute | solution.py:42
  69.8 0.9 shard_map.103
  70.7 0.7 copy-done.10
  71.3 2.6 %collective-permute-start.3 = (bf16[128,2560]{1,0:T(8,128)(2,1)}, bf16[128,2560]{1,0:T(8,128)(2,1)}, u32[]{:S(2)}, u32[]{:S(2)}) collective-permute-start(bf16[128,2560]{1,0:T(8,128)(2,1)} %shard_map.103), channel_id=1, source_target_pairs={{8,0},{9,1},{10,2},{11,3},{12,4},{13,5},{14,6},{15,7},{0,8},{1,9},... | collective-permute-start | bytes 1966088 | tf_op jit(solution)/shard_map/ppermute | solution.py:42
  73.9 0.1 cosine_multiply_fusion
  74.0 0.1 mul.64.cos_ref
  74.1 0.0 copy-done.14
  74.1 0.0 copy-done.1
  74.1 0.0 copy-start.12
  74.1 0.7 copy-done.12
  74.9 1.9 %shard_map.100 = (bf16[8,256,1024]{2,1,0:T(8,128)(2,1)S(1)}, bf16[8,256,1024]{2,1,0:T(8,128)(2,1)S(1)}, f32[16,256]{1,0:T(8,128)S(1)}, f32[8,512]{1,0:T(8,128)S(1)}) custom-call(f32[16]{0:T(128)S(1)} %mul.64.cos_ref, s32[32]{0:T(128)S(1)} %copy-done.13, s32[64]{0:T(128)S(1)} %copy-done.14, bf16[256,1024]{1,0:T(8,128)(2,1)S(1)} %copy-done, ...), custom_call_target="tpu_custom_call" | custom-call | flops 100000000 | bytes 10000000 | tf_op jit(solution)/shard_map/pallas_call | solution.py:160
  76.8 0.0 collective-permute-done.10.refs_2_
  76.8 1.0 copy-done.5
  77.8 3.1 %shard_map.107.refs_3_ = f32[2,256,512]{2,1,0:T(8,128)S(1)} custom-call(f32[16,256]{1,0:T(8,128)S(1)} %get-tuple-element.16.cos_ref, f32[8,512]{1,0:T(8,128)S(1)} %get-tuple-element.17.kept_ref, bf16[8,256,1024]{2,1,0:T(8,128)(2,1)S(1)} %get-tuple-element.18.occ_ref, bf16[8,256,1024]{2,1,0:T(8,128)(2,1)S(1)} %get-tuple-element.19.vir_ref, ...), custom_call_target="tpu_custom_call" | custom-call | flops 2147483648 | bytes 10000000 | tf_op jit(solution)/shard_map/pallas_call | solution.py:223
  81.0 3.1 %shard_map.108.refs_3_ = f32[2,256,512]{2,1,0:T(8,128)S(1)} custom-call(f32[16,256]{1,0:T(8,128)S(1)} %get-tuple-element.16.cos_ref, f32[8,512]{1,0:T(8,128)S(1)} %get-tuple-element.17.kept_ref, bf16[8,256,1024]{2,1,0:T(8,128)(2,1)S(1)} %get-tuple-element.18.occ_ref, bf16[8,256,1024]{2,1,0:T(8,128)(2,1)S(1)} %get-tuple-element.19.vir_ref, ...), custom_call_target="tpu_custom_call" | custom-call | flops 2147483648 | bytes 10000000 | tf_op jit(solution)/shard_map/pallas_call | solution.py:223
  84.1 0.0 collective-permute-done.6.refs_2_
  84.2 4.3 %shard_map.109.refs_4_ = f32[2,256,512]{2,1,0:T(8,128)S(1)} custom-call(f32[16,256]{1,0:T(8,128)S(1)} %get-tuple-element.16.cos_ref, f32[8,512]{1,0:T(8,128)S(1)} %get-tuple-element.17.kept_ref, bf16[8,256,1024]{2,1,0:T(8,128)(2,1)S(1)} %get-tuple-element.18.occ_ref, bf16[8,256,1024]{2,1,0:T(8,128)(2,1)S(1)} %get-tuple-element.19.vir_ref, ...), custom_call_target="tpu_custom_call" | custom-call | flops 2147483648 | bytes 10000000 | tf_op jit(solution)/shard_map/pallas_call | solution.py:223
  88.4 0.0 collective-permute-done.3.refs_3_
  88.4 0.0 copy-done.11
  88.4 4.3 %shard_map.110 = bf16[8,2,64,256]{3,2,1,0:T(8,128)(2,1)S(1)} custom-call(f32[16,256]{1,0:T(8,128)S(1)} %get-tuple-element.16.cos_ref, f32[8,512]{1,0:T(8,128)S(1)} %get-tuple-element.17.kept_ref, bf16[8,256,1024]{2,1,0:T(8,128)(2,1)S(1)} %get-tuple-element.18.occ_ref, bf16[8,256,1024]{2,1,0:T(8,128)(2,1)S(1)} %get-tuple-element.19.vir_ref, ...), custom_call_target="tpu_custom_call" | custom-call | flops 2147483648 | bytes 10000000 | tf_op jit(solution)/shard_map/pallas_call | solution.py:223
  92.7 14.0 %all_to_all.5 = bf16[8,2,64,256]{3,2,1,0:T(8,128)(2,1)S(1)} all-to-all(bf16[8,2,64,256]{3,2,1,0:T(8,128)(2,1)S(1)} %shard_map.110), channel_id=1, replica_groups=mesh['pts'=32,'grp'=8] {'grp'}, dimensions={0} | all-to-all | bytes 1048576 | tf_op jit(solution)/shard_map/all_to_all | solution.py:292
  106.7 0.7 convert_reduce_fusion
  (33 shorter events, 0.1 us)
Async XLA Ops:
  0.0 74.1 %copy-start.14 = (s32[64]{0:T(128)S(1)}, s32[64]{0:T(128)}, u32[]{:S(2)}) copy-start(s32[64]{0:T(128)} %constant.9.planes_ref) | copy-start | bytes 772
  0.0 74.1 %copy-start = (bf16[256,1024]{1,0:T(8,128)(2,1)S(1)}, bf16[256,1024]{1,0:T(8,128)(2,1)}, u32[]{:S(2)}) copy-start(bf16[256,1024]{1,0:T(8,128)(2,1)} %occ_ref.3) | copy-start | bytes 1572868
  0.0 74.1 %copy-start.1 = (bf16[256,1024]{1,0:T(8,128)(2,1)S(1)}, bf16[256,1024]{1,0:T(8,128)(2,1)}, u32[]{:S(2)}) copy-start(bf16[256,1024]{1,0:T(8,128)(2,1)} %vir_ref.3) | copy-start | bytes 1572868
  0.0 57.5 %copy-start.16 = (f32[1024]{0:T(1024)S(1)}, f32[1024]{0:T(1024)}, u32[]{:S(2)}) copy-start(f32[1024]{0:T(1024)} %param.14) | copy-start | bytes 12292
  0.0 57.5 %copy-start.18 = (s32[8]{0:T(128)S(1)}, s32[8]{0:T(128)}, u32[]{:S(2)}) copy-start(s32[8]{0:T(128)} %param.15) | copy-start | bytes 100
  0.0 66.8 %copy-start.15 = (f32[1024]{0:T(1024)S(1)}, f32[1024]{0:T(1024)}, u32[]{:S(2)}) copy-start(f32[1024]{0:T(1024)} %param.13) | copy-start | bytes 12292
  0.0 67.5 %copy-start.19 = (f32[8]{0:T(128)S(1)}, f32[8]{0:T(128)}, u32[]{:S(2)}) copy-start(f32[8]{0:T(128)} %param.16) | copy-start | bytes 100
  0.0 74.1 %copy-start.13 = (s32[32]{0:T(128)S(1)}, s32[32]{0:T(128)}, u32[]{:S(2)}) copy-start(s32[32]{0:T(128)} %kept_ref.1) | copy-start | bytes 388
  2.5 71.4 %copy-start.17 = (f32[2]{0:T(128)S(1)}, f32[2]{0:T(128)}, u32[]{:S(2)}) copy-start(f32[2]{0:T(128)} %param.17) | copy-start | bytes 28
  2.5 1.7 %collective-permute-start.7 = (bf16[128,2560]{1,0:T(8,128)(2,1)}, bf16[128,2560]{1,0:T(8,128)(2,1)S(1)}, u32[]{:S(2)}, u32[]{:S(2)}) collective-permute-start(bf16[128,2560]{1,0:T(8,128)(2,1)} %get-tuple-element.24), channel_id=1, source_target_pairs={{0,0},{33,1},{66,2},{99,3},{132,4},{165,5},{198,6},{231,7},{8,8},{... | collective-permute-start | bytes 1966088 | tf_op jit(solution)/shard_map/ppermute | solution.py:42
  4.3 32.2 %collective-permute-start.8 = (bf16[64,2560]{1,0:T(8,128)(2,1)S(1)}, bf16[64,2560]{1,0:T(8,128)(2,1)S(1)}, u32[]{:S(2)}, u32[]{:S(2)}) collective-permute-start(bf16[64,2560]{1,0:T(8,128)(2,1)S(1)} %get-tuple-element.25), channel_id=1, source_target_pairs={{20,0},{21,1},{22,2},{23,3},{16,4},{17,5},{18,6},{19,7},{28,8},{29... | collective-permute-start | bytes 983048 | tf_op jit(solution)/shard_map/ppermute | solution.py:42
  6.5 30.0 %collective-permute-start.9 = (bf16[64,2560]{1,0:T(8,128)(2,1)S(1)}, bf16[64,2560]{1,0:T(8,128)(2,1)S(1)}, u32[]{:S(2)}, u32[]{:S(2)}) collective-permute-start(bf16[64,2560]{1,0:T(8,128)(2,1)S(1)} %get-tuple-element.26), channel_id=1, source_target_pairs={{16,0},{17,1},{18,2},{19,3},{20,4},{21,5},{22,6},{23,7},{24,8},{25... | collective-permute-start | bytes 983048 | tf_op jit(solution)/shard_map/ppermute | solution.py:42
  36.5 4.7 %copy-start.2 = (bf16[64,2560]{1,0:T(8,128)(2,1)}, bf16[64,2560]{1,0:T(8,128)(2,1)S(1)}, u32[]{:S(2)}) copy-start(bf16[64,2560]{1,0:T(8,128)(2,1)S(1)} %collective-permute-done.8.refs_2_.refs_1_) | copy-start | bytes 983044
  36.5 4.7 %copy-start.4 = (bf16[64,2560]{1,0:T(8,128)(2,1)}, bf16[64,2560]{1,0:T(8,128)(2,1)S(1)}, u32[]{:S(2)}) copy-start(bf16[64,2560]{1,0:T(8,128)(2,1)S(1)} %collective-permute-done.9.refs_1_) | copy-start | bytes 983044
  37.8 39.0 %collective-permute-start.10 = (bf16[256,2560]{1,0:T(8,128)(2,1)}, bf16[256,2560]{1,0:T(8,128)(2,1)S(1)}, u32[]{:S(2)}, u32[]{:S(2)}) collective-permute-start(bf16[256,2560]{1,0:T(8,128)(2,1)} %shard_map.106), channel_id=1, source_target_pairs={{8,0},{9,1},{10,2},{11,3},{12,4},{13,5},{14,6},{15,7},{0,8},{1,9},... | collective-permute-start | bytes 3932168 | tf_op jit(solution)/shard_map/ppermute | solution.py:42
  39.6 3.2 %collective-permute-start.4 = (bf16[64,2560]{1,0:T(8,128)(2,1)}, bf16[64,2560]{1,0:T(8,128)(2,1)S(1)}, u32[]{:S(2)}, u32[]{:S(2)}) collective-permute-start(bf16[64,2560]{1,0:T(8,128)(2,1)} %get-tuple-element.23), channel_id=1, source_target_pairs={{0,0},{33,1},{66,2},{99,3},{132,4},{165,5},{198,6},{231,7},{8,8},{... | collective-permute-start | bytes 983048 | tf_op jit(solution)/shard_map/ppermute | solution.py:42
  41.2 16.3 %collective-permute-start = (bf16[64,2560]{1,0:T(8,128)(2,1)}, bf16[64,2560]{1,0:T(8,128)(2,1)S(1)}, u32[]{:S(2)}, u32[]{:S(2)}) collective-permute-start(bf16[64,2560]{1,0:T(8,128)(2,1)} %get-tuple-element.20), channel_id=1, source_target_pairs={{0,0},{33,1},{66,2},{99,3},{132,4},{165,5},{198,6},{231,7},{8,8},{... | collective-permute-start | bytes 983048 | tf_op jit(solution)/shard_map/ppermute | solution.py:42
  42.9 21.5 %copy-start.6 = (bf16[64,2560]{1,0:T(8,128)(2,1)}, bf16[64,2560]{1,0:T(8,128)(2,1)S(1)}, u32[]{:S(2)}) copy-start(bf16[64,2560]{1,0:T(8,128)(2,1)S(1)} %collective-permute-done.4.refs_0_) | copy-start | bytes 983044
  42.9 21.5 %collective-permute-start.5 = (bf16[64,2560]{1,0:T(8,128)(2,1)S(1)}, bf16[64,2560]{1,0:T(8,128)(2,1)S(1)}, u32[]{:S(2)}, u32[]{:S(2)}) collective-permute-start(bf16[64,2560]{1,0:T(8,128)(2,1)S(1)} %collective-permute-done.4.refs_0_), channel_id=1, source_target_pairs={{16,0},{17,1},{18,2},{19,3},{20,4},{21,5},{22,6},{23,7},{24,8},{25... | collective-permute-start | bytes 983048 | tf_op jit(solution)/shard_map/ppermute | solution.py:42
  57.6 9.9 %collective-permute-start.1 = (bf16[32,2560]{1,0:T(8,128)(2,1)S(1)}, bf16[32,2560]{1,0:T(8,128)(2,1)S(1)}, u32[]{:S(2)}, u32[]{:S(2)}) collective-permute-start(bf16[32,2560]{1,0:T(8,128)(2,1)S(1)} %get-tuple-element.21), channel_id=1, source_target_pairs={{16,0},{17,1},{18,2},{19,3},{20,4},{21,5},{22,6},{23,7},{24,8},{25... | collective-permute-start | bytes 491528 | tf_op jit(solution)/shard_map/ppermute | solution.py:42
  64.4 5.4 %collective-permute-start.2 = (bf16[32,2560]{1,0:T(8,128)(2,1)S(1)}, bf16[32,2560]{1,0:T(8,128)(2,1)S(1)}, u32[]{:S(2)}, u32[]{:S(2)}) collective-permute-start(bf16[32,2560]{1,0:T(8,128)(2,1)S(1)} %get-tuple-element.22), channel_id=1, source_target_pairs={{20,0},{21,1},{22,2},{23,3},{16,4},{17,5},{18,6},{19,7},{28,8},{29... | collective-permute-start | bytes 491528 | tf_op jit(solution)/shard_map/ppermute | solution.py:42
  64.4 1.0 copy-start.8
  65.4 18.7 %collective-permute-start.6 = (bf16[128,2560]{1,0:T(8,128)(2,1)}, bf16[128,2560]{1,0:T(8,128)(2,1)}, u32[]{:S(2)}, u32[]{:S(2)}) collective-permute-start(bf16[128,2560]{1,0:T(8,128)(2,1)} %shard_map.104), channel_id=1, source_target_pairs={{8,0},{9,1},{10,2},{11,3},{12,4},{13,5},{14,6},{15,7},{0,8},{1,9},... | collective-permute-start | bytes 1966088 | tf_op jit(solution)/shard_map/ppermute | solution.py:42
  70.7 0.7 copy-start.10
  71.3 17.1 %collective-permute-start.3 = (bf16[128,2560]{1,0:T(8,128)(2,1)}, bf16[128,2560]{1,0:T(8,128)(2,1)}, u32[]{:S(2)}, u32[]{:S(2)}) collective-permute-start(bf16[128,2560]{1,0:T(8,128)(2,1)} %shard_map.103), channel_id=1, source_target_pairs={{8,0},{9,1},{10,2},{11,3},{12,4},{13,5},{14,6},{15,7},{0,8},{1,9},... | collective-permute-start | bytes 1966088 | tf_op jit(solution)/shard_map/ppermute | solution.py:42
  74.1 0.8 copy-start.12
  76.8 1.0 copy-start.5
  77.8 3.1 %copy-start.3 = (bf16[64,2560]{1,0:T(8,128)(2,1)S(1)}, bf16[64,2560]{1,0:T(8,128)(2,1)}, u32[]{:S(2)}) copy-start(bf16[64,2560]{1,0:T(8,128)(2,1)} %copy-done.2) | copy-start | bytes 983044
  80.9 3.2 %copy-start.7 = (bf16[64,2560]{1,0:T(8,128)(2,1)S(1)}, bf16[64,2560]{1,0:T(8,128)(2,1)}, u32[]{:S(2)}) copy-start(bf16[64,2560]{1,0:T(8,128)(2,1)} %copy-done.6) | copy-start | bytes 983044
  81.0 3.2 %copy-start.9 = (bf16[64,2560]{1,0:T(8,128)(2,1)S(1)}, bf16[64,2560]{1,0:T(8,128)(2,1)}, u32[]{:S(2)}) copy-start(bf16[64,2560]{1,0:T(8,128)(2,1)} %copy-done.8) | copy-start | bytes 983044
  84.1 4.3 %copy-start.11 = (bf16[32,2560]{1,0:T(8,128)(2,1)S(1)}, bf16[32,2560]{1,0:T(8,128)(2,1)}, u32[]{:S(2)}) copy-start(bf16[32,2560]{1,0:T(8,128)(2,1)} %copy-done.10) | copy-start | bytes 491524
